TPU v7x, 32 devices: a whole 2x2x4 slice. The times are simulated.
32 devices in a mesh: seq: 8 (over y, x, core), head: 4 (over z).
Axes of the slice: x: 2, y: 2, z: 4, core: 2. Of those that a mesh axis runs over, the one named last changes fastest.
Arguments:
- queries: bfloat16 [1536, 2048], P('seq', 'head'), may hold values from -6 to 6, as said below
- keys: bfloat16 [1536, 256], P('seq'), may hold values from -6 to 6, as said below
- values: bfloat16 [1536, 256], P('seq'), may hold values from -6 to 6
- out_weight: bfloat16 [2048, 8192], P('head'), may hold values from -0.25 to 0.25
- doc_lengths: int32 [48], replicated, may hold values from 1 to 384, 1536 in all
- pair_ids: int32 [48], replicated, may hold values from 0 to 23, never falling along the last dimension, each value on 1 to 3 neighbouring positions
- block_plan: int32 [32], replicated, may hold values from 0 to 31, as said below
Outputs:
- projected: bfloat16 [1536, 8192], P(('seq', 'head'))
Inputs may be any that keep to these rules, and one draw needn't show every extreme that they name: Entries of queries lie in the range given. Entries of keys lie in the range given. `doc_lengths`: the lengths sum to 1536. `pair_ids`: never falling; every pair 0 to 23 holds one to three consecutive documents. `block_plan`: A permutation of the 32 blocks of 48 tokens, numbered along the row. The 4 consecutive slots of one seq index hold blocks from 4 different seq indices, and the 4 blocks of one seq index go to 4 different seq indices.
All inputs are finite; a program needn't handle non-finite values.
Results may differ from a plain program's by a relative error of at most 0.015.
Values may be sent and summed in bfloat16 or wider, within the bound.
A program may use at most 64 MiB of HBM per device.

v0:
```python
import math
import jax
import jax.numpy as jnp
from jax import lax
from jax.sharding import PartitionSpec as P

D_HEAD = 128
NEGATIVE = -1e30


def token_docs(positions, doc_lengths):
    doc_ends = jnp.cumsum(doc_lengths)
    return jnp.sum((doc_ends[None, :] <= positions[:, None]).astype(jnp.int32), axis=1)


def pair_firsts(docs, pair_ids):
    doc_range = jnp.arange(pair_ids.shape[0], dtype=jnp.int32)
    own_pair = jnp.sum(jnp.where(docs[:, None] == doc_range[None, :], pair_ids[None, :], 0), axis=1)
    return jnp.sum((pair_ids[None, :] < own_pair[:, None]).astype(jnp.int32), axis=1)


def largest_divisor(total_rows, ceiling):
    return max(
        (
            candidate
            for candidate in range(1, min(total_rows, ceiling) + 1)
            if total_rows % candidate == 0
        )
    )


def attend(query_rows, positions, keys, values, doc_lengths, pair_ids):
    head_size = keys.shape[1]
    token_count = query_rows.shape[0]
    query_heads = query_rows.shape[1] // head_size
    shaped_queries = query_rows.reshape(token_count, query_heads, head_size)
    query_docs = token_docs(positions, doc_lengths)
    query_firsts = pair_firsts(query_docs, pair_ids)
    doc_range = jnp.arange(doc_lengths.shape[0], dtype=jnp.int32)
    pair_begin = jnp.sum(
        jnp.where(doc_range[None, :] < query_firsts[:, None], doc_lengths[None, :], 0), axis=1
    )
    lowest = jnp.min(pair_begin)
    highest = jnp.max(positions)
    scale = 1.0 / math.sqrt(head_size)

    def update(softmax_state, key_block, value_block, block_start):
        key_pos = block_start + jnp.arange(key_block.shape[0], dtype=jnp.int32)
        needed = (block_start <= highest) & (block_start + key_block.shape[0] > lowest)

        def compute(current):
            running_max, denominator, weighted = current
            key_docs = token_docs(key_pos, doc_lengths)
            allowed = (key_pos[None, :] <= positions[:, None]) & (
                (key_docs[None, :] == query_docs[:, None])
                | (key_docs[None, :] == query_firsts[:, None])
            )
            scores = (
                jnp.einsum(
                    "qhd,kd->hqk", shaped_queries, key_block, preferred_element_type=jnp.float32
                )
                * scale
            )
            newest = jnp.maximum(
                running_max, jnp.max(jnp.where(allowed[None], scores, NEGATIVE), axis=2)
            )
            weights = jnp.where(allowed[None], jnp.exp(scores - newest[:, :, None]), 0.0)
            factor = jnp.exp(running_max - newest)
            denominator = denominator * factor + jnp.sum(weights, axis=2)
            weighted = weighted * factor[:, :, None] + jnp.einsum(
                "hqk,kd->hqd",
                weights.astype(jnp.bfloat16),
                value_block,
                preferred_element_type=jnp.float32,
            )
            return (newest, denominator, weighted)

        def unchanged(current):
            return current

        return lax.cond(needed, compute, unchanged, softmax_state)

    initial = (
        jnp.full((query_heads, token_count), NEGATIVE, jnp.float32),
        jnp.zeros((query_heads, token_count), jnp.float32),
        jnp.zeros((query_heads, token_count, head_size), jnp.float32),
    )
    key_rows = lax.all_gather(keys, "seq", axis=0, tiled=True)
    value_rows = lax.all_gather(values, "seq", axis=0, tiled=True)
    row_total = key_rows.shape[0]
    block_rows = largest_divisor(row_total, 1024)
    block_count = row_total // block_rows
    stacked = (
        key_rows.reshape(block_count, block_rows, head_size),
        value_rows.reshape(block_count, block_rows, head_size),
        jnp.int32(0) + block_rows * jnp.arange(block_count, dtype=jnp.int32),
    )

    def advance(carried, block_item):
        return (update(carried, block_item[0], block_item[1], block_item[2]), None)

    result_state, unused_out = lax.scan(advance, initial, stacked)
    running_max, denominator, weighted = result_state
    attended = weighted / denominator[:, :, None]
    return (
        attended.transpose(1, 0, 2)
        .reshape(token_count, query_heads * head_size)
        .astype(jnp.bfloat16)
    )


def on_device(queries, keys, values, out_weight, doc_lengths, pair_ids, block_plan):
    seq_count = lax.axis_size("seq")
    my_seq = lax.axis_index("seq")
    shared_head = lax.axis_index("head") // 2
    key_rows = lax.dynamic_slice_in_dim(keys, shared_head * D_HEAD, D_HEAD, 1)
    value_rows = lax.dynamic_slice_in_dim(values, shared_head * D_HEAD, D_HEAD, 1)
    slots_here = seq_count // 2
    tok_rows = queries.shape[0]
    row_width = queries.shape[1]
    block_rows = tok_rows // slots_here
    slot_total = block_plan.shape[0]
    local_ids = my_seq * slots_here + jnp.arange(slots_here, dtype=jnp.int32)
    plan_rows = lax.dynamic_slice_in_dim(block_plan, my_seq * slots_here, slots_here, 0)
    planned_pos = (
        plan_rows[:, None] * block_rows + jnp.arange(block_rows, dtype=jnp.int32)[None, :]
    ).reshape(-1)
    slot_range = jnp.arange(slot_total, dtype=jnp.int32)
    target_slot = jnp.sum(
        jnp.where(block_plan[None, :] == local_ids[:, None], slot_range[None, :], 0), axis=1
    )
    device_range = jnp.arange(seq_count, dtype=jnp.int32)
    send_table = ((target_slot // slots_here)[:, None] == device_range[None, :]).astype(
        jnp.bfloat16
    )
    take_table = ((plan_rows // slots_here)[:, None] == device_range[None, :]).astype(jnp.bfloat16)
    blocked = queries.reshape(slots_here, block_rows, row_width)
    arrived = lax.all_to_all(
        jnp.einsum("bn,bkw->nkw", send_table, blocked, preferred_element_type=jnp.float32).astype(
            jnp.bfloat16
        ),
        "seq",
        split_axis=0,
        concat_axis=0,
        tiled=True,
    )
    chosen = jnp.einsum("bn,nkw->bkw", take_table, arrived, preferred_element_type=jnp.float32)
    attended = attend(
        chosen.astype(jnp.bfloat16).reshape(tok_rows, row_width),
        planned_pos,
        key_rows,
        value_rows,
        doc_lengths,
        pair_ids,
    )
    return lax.psum_scatter(
        jnp.dot(attended, out_weight, preferred_element_type=jnp.float32).astype(jnp.bfloat16),
        "head",
        scatter_dimension=0,
        tiled=True,
    )


def solution(mesh):
    return jax.shard_map(
        on_device,
        mesh=mesh,
        in_specs=(P("seq", "head"), P("seq", None), P("seq", None), P("head", None), P(), P(), P()),
        out_specs=P(("seq", "head"), None),
        check_vma=False,
    )
```

profile of v0, /device:TPU:0, one launch (start us, length us, event | category | flops | bytes accessed | tf_op | source)
XLA Modules:
  0.0 128.1 jit_solution(16628329436122712984)
XLA Ops:
  6.5 0.0 copy-start
  6.5 0.0 copy-start.2
  6.5 0.0 copy-start.3
  6.5 0.9 select_reduce_fusion.2
  7.4 0.0 copy-done
  7.5 0.4 convolution_convert_fusion.1
  7.9 0.0 copy-start.1
  7.9 0.9 copy.26
  8.7 5.2 %all-to-all-start = ((bf16[8,48,512]{2,1,0:T(8,128)(2,1)}), bf16[8,48,512]{2,1,0:T(8,128)(2,1)S(1)}, u32[]{:S(2)}, u32[]{:S(2)}) async-start(bf16[8,48,512]{2,1,0:T(8,128)(2,1)} %copy.26), calls=%async_computation | async-start | bytes 786432 | tf_op jit(solution)/shard_map/all_to_all | solution.py:138
  13.9 0.0 reduce-scatter.2.cloned.1.call-start
  14.0 0.7 and_select_fusion.1
  14.7 0.8 iota_add_fusion
  15.5 0.1 add.80
  15.6 0.7 copy.24
  16.3 0.1 reduce-window.17
  16.4 0.1 reduce.2
  16.5 0.1 convert_reduce_fusion.2
  16.6 0.7 select_reduce_fusion.1
  17.4 0.7 convert_reduce_fusion.1
  18.1 0.7 select_reduce_fusion
  18.9 0.0 copy-done.2
  18.9 10.0 %all_gather.7 = bf16[1536,128]{1,0:T(8,128)(2,1)S(1)} all-gather(bf16[192,128]{1,0:T(8,128)(2,1)S(1)} %constant_dynamic-slice_fusion), channel_id=1, replica_groups=mesh['seq'=8,'head'=4] {'seq'}, dimensions={0}, use_global_device_ids=true | all-gather | bytes 442368 | tf_op jit(solution)/shard_map/all_gather | solution.py:89
  28.9 0.6 reduce_min.9
  29.5 0.0 copy-done.3
  29.6 9.5 %all_gather.6 = bf16[1536,128]{1,0:T(8,128)(2,1)S(1)} all-gather(bf16[192,128]{1,0:T(8,128)(2,1)S(1)} %constant_dynamic-slice_fusion.1), channel_id=1, replica_groups=mesh['seq'=8,'head'=4] {'seq'}, dimensions={0}, use_global_device_ids=true | all-gather | bytes 442368 | tf_op jit(solution)/shard_map/all_gather | solution.py:88
  39.1 0.0 all-to-all-done
  39.1 0.4 convolution_convert_fusion.2
  39.5 0.1 reshape_reshape.3
  39.6 0.0 copy-done.1
  39.6 13.9 %while.15 = (s32[]{:T(128)}, f32[4,192]{1,0:T(4,128)S(1)}, f32[4,192]{1,0:T(4,128)S(1)}, f32[4,192,128]{2,1,0:T(8,128)S(1)}, s32[2]{0:T(128)S(1)}, /*index=5*/s3...) while((s32[]{:T(128)}, f32[4,192]{1,0:T(4,128)S(1)}, ...), condition=%wide.region_15.16_spmd.clone, body=%wide.region_8.15_spmd.clone.sunk | while | flops 309526400 | bytes 9124563 | solution.py:102
  39.7 0.6 dynamic_slice.49
  42.8 3.8 %conditional.3 = ((f32[4,192]{1,0:T(4,128)S(1)}, f32[4,192]{1,0:T(4,128)S(1)}, f32[4,192,128]{2,1,0:T(8,128)S(1)})) conditional(s32[]{:T(128)} %convert_element_type.62, (f32[4,192]{1,0:T(4,128)S(1)}, f32[4,192]{1,0:T(4,128)S(1)}, f32[4,192,128]{2,1,0:T(8,128)S(1)}) %tuple.43, (s32[]{:T(128)}, s32[768]{0:T(1024)S(1)}, s32[4]{0:T(128)S(1)}, ...), branch_computations={%region_9.9_spmd, %region_10.14_spmd} | conditional | flops 309526400 | bytes 9120388 | solution.py:81
  42.8 0.7 broadcast_add_fusion
  43.5 0.1 copy.23
  43.6 0.1 reduce-window.15
  43.6 0.1 reduce.1
  43.8 0.1 convert_reduce_fusion
  43.9 0.1 broadcast_add_fusion.1
  43.9 0.1 le.47
  44.0 0.2 or_and_fusion
  44.2 0.7 fusion.2
  44.9 0.8 fusion.6
  45.7 0.8 convolution_add_fusion
  46.6 0.6 dynamic_slice.49
  49.7 3.8 %conditional.3 = ((f32[4,192]{1,0:T(4,128)S(1)}, f32[4,192]{1,0:T(4,128)S(1)}, f32[4,192,128]{2,1,0:T(8,128)S(1)})) conditional(s32[]{:T(128)} %convert_element_type.62, (f32[4,192]{1,0:T(4,128)S(1)}, f32[4,192]{1,0:T(4,128)S(1)}, f32[4,192,128]{2,1,0:T(8,128)S(1)}) %tuple.43, (s32[]{:T(128)}, s32[768]{0:T(1024)S(1)}, s32[4]{0:T(128)S(1)}, ...), branch_computations={%region_9.9_spmd, %region_10.14_spmd} | conditional | flops 309526400 | bytes 9120388 | solution.py:81
  49.8 0.7 broadcast_add_fusion
  50.4 0.1 copy.23
  50.5 0.1 reduce-window.15
  50.6 0.1 reduce.1
  50.7 0.1 convert_reduce_fusion
  50.8 0.1 broadcast_add_fusion.1
  50.9 0.1 le.47
  51.0 0.2 or_and_fusion
  51.2 0.7 fusion.2
  51.9 0.8 fusion.6
  52.6 0.8 convolution_add_fusion
  53.5 6.9 %convolution_convert_fusion = bf16[192,8192]{1,0:T(8,128)(2,1)} fusion(bf16[512,8192]{1,0:T(8,128)(2,1)} %param.14, f32[4,192,128]{2,1,0:T(8,128)S(1)} %get-tuple-element.191, f32[4,192]{1,0:T(4,128)S(1)} %get-tuple-element.192), kind=kOutput, calls=%fused_computation.27 | convolution fusion | flops 1612382208 | bytes 11930624 | tf_op jit(solution)/shard_map/dot_general | solution.py:157
  60.4 0.0 reduce-scatter.2.cloned.1.call-update
  60.4 60.8 %reduce-scatter.2.cloned.1.call-done = bf16[48,8192]{1,0:T(8,128)(2,1)} async-done(((bf16[192,8192]{1,0:T(8,128)(2,1)}), bf16[48,8192]{1,0:T(8,128)(2,1)}) %reduce-scatter.2.cloned.1.call-update) | async-done | bytes 786448 | tf_op jit(solution)/shard_map/reduce_scatter | solution.py:156
  (20 shorter events, 0.2 us)
Async XLA Ops:
  6.5 0.9 copy-start
  6.5 12.3 %copy-start.2 = (bf16[192,256]{1,0:T(8,128)(2,1)S(1)}, bf16[192,256]{1,0:T(8,128)(2,1)}, u32[]{:S(2)}) copy-start(bf16[192,256]{1,0:T(8,128)(2,1)} %param.13) | copy-start | bytes 294916
  6.5 23.0 %copy-start.3 = (bf16[192,256]{1,0:T(8,128)(2,1)S(1)}, bf16[192,256]{1,0:T(8,128)(2,1)}, u32[]{:S(2)}) copy-start(bf16[192,256]{1,0:T(8,128)(2,1)} %param.12) | copy-start | bytes 294916
  7.9 31.8 %copy-start.1 = (s32[48]{0:T(128)S(1)}, s32[48]{0:T(128)}, u32[]{:S(2)}) copy-start(s32[48]{0:T(128)} %param.15) | copy-start | bytes 580
  8.7 30.3 %all-to-all-start = ((bf16[8,48,512]{2,1,0:T(8,128)(2,1)}), bf16[8,48,512]{2,1,0:T(8,128)(2,1)S(1)}, u32[]{:S(2)}, u32[]{:S(2)}) async-start(bf16[8,48,512]{2,1,0:T(8,128)(2,1)} %copy.26), calls=%async_computation | async-start | bytes 786432 | tf_op jit(solution)/shard_map/all_to_all | solution.py:138
  13.9 107.4 %reduce-scatter.2.cloned.1.call-start = ((), (), s32[]{:S(2)}) async-start(), calls=%async_computation.2 | async-start | bytes 3932160 | tf_op jit(solution)/shard_map/reduce_scatter | solution.py:156
Sparse Core Ops, SparseCore 0:
  60.6 60.6 reduce-scatter.1
where the time goes:
time: 129 us; the launch traced here: 128 us
  waiting for transfers between devices  60.9 us (47%)
  blocking collectives  19.5 us (15%)
  between operations  13.5 us (10%)
  matrix products  10.7 us (8%)
  other arithmetic  9.6 us (7%)
  loops' own time  5.26 us (4%)
  starting transfers between devices  5.23 us (4%)
  local copies, waits for them, and re-layouts  3.44 us (3%)
    reduce_scatter x1, waiting for transfers between devices, on_device(): lax.psum_scatter(jnp.dot(attended, out_weight, preferred_element_type=jnp...  60.8 us
    all_gather x1, blocking collectives, attend(): value_rows = lax.all_gather(values, 'seq', axis=0, tiled=True)  10 us
    all_gather x1, blocking collectives, attend(): key_rows = lax.all_gather(keys, 'seq', axis=0, tiled=True)  9.51 us
    dot_general x1, matrix products, on_device(): jnp.dot(attended, out_weight, preferred_element_type=jnp.float32)  6.91 us
    all_to_all x1, starting transfers between devices, on_device(): lax.all_to_all(jnp.einsum('bn,bkw->nkw', send_table, blocked, preferred_e...  5.2 us
    another operation x1, loops' own time, attend(): result_state, unused_out = lax.scan(advance, initial, stacked)  5.15 us
  transfers between devices with their start and end apart: 2, of which 1 were waited for; matrix products, arithmetic and copies ran while one was open for 4% of the time, Pallas kernels for 0%

commit v1 on v0

--- a/solution.py
+++ b/solution.py
@@ -85,8 +85,11 @@
         jnp.zeros((query_heads, token_count), jnp.float32),
         jnp.zeros((query_heads, token_count, head_size), jnp.float32),
     )
-    key_rows = lax.all_gather(keys, "seq", axis=0, tiled=True)
-    value_rows = lax.all_gather(values, "seq", axis=0, tiled=True)
+    key_rows, value_rows = jnp.split(
+        lax.all_gather(jnp.concatenate([keys, values], axis=1), "seq", axis=0, tiled=True),
+        [keys.shape[1]],
+        axis=1,
+    )
     row_total = key_rows.shape[0]
     block_rows = largest_divisor(row_total, 1024)
     block_count = row_total // block_rows

time: 129 us -> 120 us (0.930)
  blocking collectives: 19.5 us -> 12.9 us
  other arithmetic: 9.6 us -> 7.02 us
    all_gather x2 -> x1, blocking collectives: 19.5 us -> 12.9 us  [attend(): lax.all_gather(jnp.concatenate([keys, values], axis=1), 'seq', axis=0, ti...]
  transfers between devices with their start and end apart: 2 -> 2, of which waited for: 1 -> 1; matrix products, arithmetic and copies ran while one was open for 4% -> 3% of each run, Pallas kernels for 0% -> 0%
where the time goes in v1:
time: 120 us; the launch traced here: 119 us
  waiting for transfers between devices  60.9 us (51%)
  between operations  13.5 us (11%)
  blocking collectives  12.9 us (11%)
  matrix products  10.7 us (9%)
  other arithmetic  7.02 us (6%)
  loops' own time  5.26 us (4%)
  starting transfers between devices  5.23 us (4%)
  local copies, waits for them, and re-layouts  3.65 us (3%)
    reduce_scatter x1, waiting for transfers between devices, on_device(): lax.psum_scatter(jnp.dot(attended, out_weight, preferred_element_type=jnp...  60.8 us
    all_gather x1, blocking collectives, attend(): lax.all_gather(jnp.concatenate([keys, values], axis=1), 'seq', axis=0, ti...  12.9 us
    dot_general x1, matrix products, on_device(): jnp.dot(attended, out_weight, preferred_element_type=jnp.float32)  6.91 us
    all_to_all x1, starting transfers between devices, on_device(): lax.all_to_all(jnp.einsum('bn,bkw->nkw', send_table, blocked, preferred_e...  5.2 us
    another operation x1, loops' own time, attend(): result_state, unused_out = lax.scan(advance, initial, stacked)  5.15 us
  transfers between devices with their start and end apart: 2, of which 1 were waited for; matrix products, arithmetic and copies ran while one was open for 3% of the time, Pallas kernels for 0%

profile of v1, /device:TPU:0, one launch (start us, length us, event | category | flops | bytes accessed | tf_op | source)
XLA Modules:
  0.0 119.2 jit_solution(6583112105385251287)
XLA Ops:
  6.5 0.0 copy-start
  6.5 0.0 copy-start.3
  6.5 0.0 copy-start.1
  6.5 0.0 copy-start.2
  6.5 0.9 select_reduce_fusion.2
  7.5 0.0 copy-done
  7.5 0.4 convolution_convert_fusion.1
  7.9 0.9 copy.26
  8.7 5.2 %all-to-all-start = ((bf16[8,48,512]{2,1,0:T(8,128)(2,1)}), bf16[8,48,512]{2,1,0:T(8,128)(2,1)S(1)}, u32[]{:S(2)}, u32[]{:S(2)}) async-start(bf16[8,48,512]{2,1,0:T(8,128)(2,1)} %copy.26), calls=%async_computation | async-start | bytes 786432 | tf_op jit(solution)/shard_map/all_to_all | solution.py:141
  13.9 0.0 reduce-scatter.2.cloned.1.call-start
  14.0 0.8 constant_dynamic-slice_fusion
  14.8 12.9 %all_gather.3 = bf16[1536,256]{1,0:T(8,128)(2,1)S(1)} all-gather(bf16[192,256]{1,0:T(8,128)(2,1)S(1)} %pad_maximum_fusion), channel_id=1, replica_groups=mesh['seq'=8,'head'=4] {'seq'}, dimensions={0}, use_global_device_ids=true | all-gather | bytes 884736 | tf_op jit(solution)/shard_map/all_gather | solution.py:89
  27.7 0.0 copy-done.3
  27.7 0.1 and_select_fusion.1
  27.8 0.8 iota_add_fusion
  28.6 0.1 add.80
  28.7 0.0 copy-done.1
  28.7 0.1 copy.24
  28.8 0.1 reduce-window.17
  28.9 0.1 reduce.2
  29.0 0.1 convert_reduce_fusion.2
  29.1 0.0 copy-done.2
  29.1 0.1 select_reduce_fusion.1
  29.2 0.1 convert_reduce_fusion.1
  29.3 0.1 select_reduce_fusion
  29.4 0.6 reduce_min.9
  30.0 0.1 fusion.32
  30.1 0.0 all-to-all-done
  30.1 0.4 convolution_convert_fusion.2
  30.5 0.1 reshape_reshape.3
  30.6 13.9 %while.15 = (s32[]{:T(128)}, f32[4,192]{1,0:T(4,128)S(1)}, f32[4,192]{1,0:T(4,128)S(1)}, f32[4,192,128]{2,1,0:T(8,128)S(1)}, s32[2]{0:T(128)S(1)}, /*index=5*/s3...) while((s32[]{:T(128)}, f32[4,192]{1,0:T(4,128)S(1)}, ...), condition=%wide.region_15.16_spmd.clone, body=%wide.region_8.15_spmd.clone.sunk | while | flops 309526400 | bytes 9124563 | solution.py:105
  30.6 0.6 dynamic_slice.49
  33.8 3.8 %conditional.3 = ((f32[4,192]{1,0:T(4,128)S(1)}, f32[4,192]{1,0:T(4,128)S(1)}, f32[4,192,128]{2,1,0:T(8,128)S(1)})) conditional(s32[]{:T(128)} %convert_element_type.62, (f32[4,192]{1,0:T(4,128)S(1)}, f32[4,192]{1,0:T(4,128)S(1)}, f32[4,192,128]{2,1,0:T(8,128)S(1)}) %tuple.45, (s32[]{:T(128)}, s32[768]{0:T(1024)S(1)}, s32[4]{0:T(128)S(1)}, ...), branch_computations={%region_9.9_spmd, %region_10.14_spmd} | conditional | flops 309526400 | bytes 9120388 | solution.py:81
  33.8 0.7 broadcast_add_fusion
  34.5 0.1 copy.23
  34.6 0.1 reduce-window.15
  34.6 0.1 reduce.1
  34.7 0.1 convert_reduce_fusion
  34.8 0.1 broadcast_add_fusion.1
  34.9 0.1 le.47
  35.0 0.2 or_and_fusion
  35.2 0.7 fusion.2
  35.9 0.8 fusion.6
  36.7 0.9 convolution_add_fusion
  37.6 0.6 dynamic_slice.49
  40.7 3.8 %conditional.3 = ((f32[4,192]{1,0:T(4,128)S(1)}, f32[4,192]{1,0:T(4,128)S(1)}, f32[4,192,128]{2,1,0:T(8,128)S(1)})) conditional(s32[]{:T(128)} %convert_element_type.62, (f32[4,192]{1,0:T(4,128)S(1)}, f32[4,192]{1,0:T(4,128)S(1)}, f32[4,192,128]{2,1,0:T(8,128)S(1)}) %tuple.45, (s32[]{:T(128)}, s32[768]{0:T(1024)S(1)}, s32[4]{0:T(128)S(1)}, ...), branch_computations={%region_9.9_spmd, %region_10.14_spmd} | conditional | flops 309526400 | bytes 9120388 | solution.py:81
  40.8 0.7 broadcast_add_fusion
  41.4 0.1 copy.23
  41.5 0.1 reduce-window.15
  41.6 0.1 reduce.1
  41.7 0.1 convert_reduce_fusion
  41.8 0.1 broadcast_add_fusion.1
  41.9 0.1 le.47
  42.0 0.2 or_and_fusion
  42.2 0.7 fusion.2
  42.9 0.8 fusion.6
  43.7 0.9 convolution_add_fusion
  44.6 6.9 %convolution_convert_fusion = bf16[192,8192]{1,0:T(8,128)(2,1)} fusion(bf16[512,8192]{1,0:T(8,128)(2,1)} %param.14, f32[4,192,128]{2,1,0:T(8,128)S(1)} %get-tuple-element.191, f32[4,192]{1,0:T(4,128)S(1)} %get-tuple-element.192), kind=kOutput, calls=%fused_computation.27 | convolution fusion | flops 1612382208 | bytes 11930624 | tf_op jit(solution)/shard_map/dot_general | solution.py:160
  51.5 0.0 reduce-scatter.2.cloned.1.call-update
  51.5 60.8 %reduce-scatter.2.cloned.1.call-done = bf16[48,8192]{1,0:T(8,128)(2,1)} async-done(((bf16[192,8192]{1,0:T(8,128)(2,1)}), bf16[48,8192]{1,0:T(8,128)(2,1)}) %reduce-scatter.2.cloned.1.call-update) | async-done | bytes 786448 | tf_op jit(solution)/shard_map/reduce_scatter | solution.py:159
  (19 shorter events, 0.2 us)
Async XLA Ops:
  6.5 0.9 copy-start
  6.5 21.2 %copy-start.3 = (s32[32]{0:T(128)S(1)}, s32[32]{0:T(128)}, u32[]{:S(2)}) copy-start(s32[32]{0:T(128)} %param.17) | copy-start | bytes 388
  6.5 22.2 %copy-start.1 = (s32[48]{0:T(128)S(1)}, s32[48]{0:T(128)}, u32[]{:S(2)}) copy-start(s32[48]{0:T(128)} %param.15) | copy-start | bytes 580
  6.5 22.5 %copy-start.2 = (s32[48]{0:T(128)S(1)}, s32[48]{0:T(128)}, u32[]{:S(2)}) copy-start(s32[48]{0:T(128)} %param.16) | copy-start | bytes 580
  8.7 21.3 %all-to-all-start = ((bf16[8,48,512]{2,1,0:T(8,128)(2,1)}), bf16[8,48,512]{2,1,0:T(8,128)(2,1)S(1)}, u32[]{:S(2)}, u32[]{:S(2)}) async-start(bf16[8,48,512]{2,1,0:T(8,128)(2,1)} %copy.26), calls=%async_computation | async-start | bytes 786432 | tf_op jit(solution)/shard_map/all_to_all | solution.py:141
  13.9 98.4 %reduce-scatter.2.cloned.1.call-start = ((), (), s32[]{:S(2)}) async-start(), calls=%async_computation.2 | async-start | bytes 3932160 | tf_op jit(solution)/shard_map/reduce_scatter | solution.py:159
Sparse Core Ops, SparseCore 0:
  51.6 60.6 reduce-scatter.1
